TPU v7x, 128 devices: a whole 4x4x4 slice. The times are simulated.
128 devices in a mesh: group: 32 (over z, y, core), local: 4 (over x).
Axes of the slice: x: 4, y: 4, z: 4, core: 2. Of those that a mesh axis runs over, the one named last changes fastest.
Arguments:
- dense_vec: bfloat16 [16384, 128], P(('group', 'local')), may hold values from -6 to 6
- q_tables: float32 [4096, 26, 128], P('group'), may hold values from -4 to 4
- r_tables: float32 [256, 26, 128], P('local'), may hold values from -4 to 4
- owner: int32 [16384, 26, 1], P(('group', 'local')), may hold values from 0 to 31; in each aligned block of 3328 rows (0 to 3327, 3328 to 6655, ..., all dimensions but the last counted through in order) at most 208 rows name the same one
- q_local: int32 [16384, 26], P(('group', 'local')), may hold values from 0 to 127
- r_index: int32 [16384, 26], P(('group', 'local')), may hold values from 0 to 255
- w_one: bfloat16 [479, 1024], replicated, may hold values from -0.25 to 0.25
- b_one: float32 [1024], replicated, may hold values from -3 to 3
- w_two: bfloat16 [1024, 1024], replicated, may hold values from -0.1875 to 0.1875
- b_two: float32 [1024], replicated, may hold values from -3 to 3
- w_three: bfloat16 [1024, 512], replicated, may hold values from -0.1875 to 0.1875
- b_three: float32 [512], replicated, may hold values from -3 to 3
- w_four: bfloat16 [512, 256], replicated, may hold values from -0.25 to 0.25
- b_four: float32 [256], replicated, may hold values from -3 to 3
- cotangent: bfloat16 [16384, 256], P(('group', 'local')), may hold values from -6 to 6
Outputs:
- q_new: float32 [4096, 26, 128], P('group')
- r_new: float32 [256, 26, 128], P('local')
- w_one_new: float32 [479, 1024], replicated
- b_one_new: float32 [1024], replicated
- w_two_new: float32 [1024, 1024], replicated
- b_two_new: float32 [1024], replicated
- w_three_new: float32 [1024, 512], replicated
- b_three_new: float32 [512], replicated
- w_four_new: float32 [512, 256], replicated
- b_four_new: float32 [256], replicated
Inputs may be any that keep to these rules, and one draw needn't show every extreme that they name: `owner`: within the rows of one device (its 128 samples times 26 tables), no group is named more than 208 times, a bound that some block reaches.
All inputs are finite; a program needn't handle non-finite values.
Results may differ from a plain program's by a relative error of at most 0.0025.
Values may be sent and summed in bfloat16 or wider, within the bound.
No kernel may reach another device: no remote copies, remote signals or barrier semaphores. Data moves between devices by JAX's collectives and lax.ppermute only.
A program may use at most 128 MiB of HBM per device.

v0:
```python
import jax
import jax.numpy as jnp
import numpy as np
from jax import lax
from jax.sharding import PartitionSpec as P

table_rate = 0.05
dense_rate = 0.0005


def cut_along(array, dim, length):
    before, after = (array.shape[:dim], array.shape[dim + 1 :])
    return jnp.moveaxis(array.reshape(*before, length, -1, *after), dim, 0)


def summed_on_arrival(array, axis, dim):
    blocks = cut_along(array, dim, lax.axis_size(axis))
    arrived = lax.all_to_all(blocks, axis, split_axis=0, concat_axis=0, tiled=True)
    return arrived.astype(jnp.float32).sum(axis=0)


def in_order(blocks, dim):
    shape = list(blocks.shape[1:])
    shape[dim] *= blocks.shape[0]
    return jnp.moveaxis(blocks, 0, dim).reshape(shape)


def sent_to_all(array, axis):
    length = lax.axis_size(axis)
    return lax.all_to_all(
        jnp.broadcast_to(array[None], (length, *array.shape)), axis, 0, 0, tiled=True
    )


def gather_directly(array, axis, dim):
    return in_order(sent_to_all(array, axis), dim)


def silu_slope(preact):
    sigma = jax.nn.sigmoid(preact)
    return sigma * (1.0 + preact * (1.0 - sigma))


def interact(dense_rows, embeds):
    vectors_all = jnp.concatenate([dense_rows[:, None, :], embeds], axis=1).astype(jnp.float32)
    gram_mat = jnp.einsum("bid,bjd->bij", vectors_all, vectors_all, precision=lax.Precision.HIGHEST)
    lower_i, lower_j = np.tril_indices(vectors_all.shape[1], -1)
    pair_vals = gram_mat[:, lower_i, lower_j]
    features = jnp.concatenate([dense_rows.astype(jnp.float32), pair_vals], axis=1).astype(
        jnp.bfloat16
    )
    return (vectors_all, features)


def pair_back(d_pairs, vectors_all):
    vectors = vectors_all.shape[1]
    lower_i, lower_j = np.tril_indices(vectors, -1)
    spread = (
        jnp.zeros((vectors_all.shape[0], vectors, vectors), jnp.float32)
        .at[:, lower_i, lower_j]
        .set(d_pairs)
    )
    spread = spread + jnp.swapaxes(spread, 1, 2)
    return jnp.einsum("bij,bjd->bid", spread, vectors_all, precision=lax.Precision.HIGHEST)


def contract_rows(left, right):
    return lax.dot_general(
        left, right, (((0,), (0,)), ((), ())), preferred_element_type=jnp.float32
    )


def dense_pass(features, layers, cot_rows):
    inputs_list = [features]
    pre_list = []
    current = features
    for layer_idx, (weight, biases) in enumerate(layers):
        pre_act = jnp.dot(current, weight, preferred_element_type=jnp.float32) + biases
        pre_list.append(pre_act)
        if layer_idx + 1 < len(layers):
            current = jax.nn.silu(pre_act).astype(jnp.bfloat16)
            inputs_list.append(current)
    grad_low = cot_rows
    grad_full = cot_rows.astype(jnp.float32)
    grads = []
    back_grad = None
    for layer_idx in reversed(range(len(layers))):
        weight = layers[layer_idx][0]
        w_grad = contract_rows(inputs_list[layer_idx], grad_low)
        b_grad = jnp.sum(grad_full, axis=0)
        back_grad = lax.dot_general(
            grad_low, weight, (((1,), (1,)), ((), ())), preferred_element_type=jnp.float32
        )
        grads.insert(0, (w_grad, b_grad))
        if layer_idx > 0:
            grad_full = back_grad * silu_slope(pre_list[layer_idx - 1])
            grad_low = grad_full.astype(jnp.bfloat16)
    return (grads, back_grad)


def body(
    dense_vec,
    q_tables,
    r_tables,
    owner,
    q_local,
    r_index,
    w_one,
    b_one,
    w_two,
    b_two,
    w_three,
    b_three,
    w_four,
    b_four,
    cotangent,
):
    layers = [(w_one, b_one), (w_two, b_two), (w_three, b_three), (w_four, b_four)]
    groups = lax.axis_size("group")
    batch_rows, table_count = q_local.shape
    embed_width = q_tables.shape[2]
    lookups = batch_rows * table_count
    capacity = 2 * lookups // groups
    slot_count = groups * capacity
    segment_count = q_tables.shape[0] * table_count
    table_ids = jnp.arange(table_count, dtype=jnp.int32)[None, :]
    highest = lax.Precision.HIGHEST
    dest_group = owner[:, :, 0]
    owner_hits = (
        dest_group[:, :, None] == jnp.arange(groups, dtype=jnp.int32)[None, None, :]
    ).astype(jnp.float32)
    table_lower = (jnp.arange(table_count)[:, None] < jnp.arange(table_count)[None, :]).astype(
        jnp.float32
    )
    sample_lower = (jnp.arange(batch_rows)[:, None] < jnp.arange(batch_rows)[None, :]).astype(
        jnp.float32
    )
    within = jnp.einsum("st,bsg->btg", table_lower, owner_hits, precision=highest)
    before = jnp.einsum("cb,cg->bg", sample_lower, jnp.sum(owner_hits, axis=1), precision=highest)
    slot_rank = jnp.sum((within + before[:, None, :]) * owner_hits, axis=2).astype(jnp.int32)
    position = (dest_group * capacity + slot_rank).reshape(lookups)
    source = (
        jnp.full((slot_count,), lookups, jnp.int32)
        .at[position]
        .set(jnp.arange(lookups, dtype=jnp.int32))
    )
    row_keys = (q_local * table_count + table_ids).reshape(lookups)
    keys_padded = jnp.concatenate([row_keys, jnp.zeros((1,), jnp.int32)])
    outgoing = keys_padded[source].reshape(groups, capacity)
    flat_table = q_tables.reshape(segment_count, embed_width)
    request = lax.all_to_all(outgoing, "group", split_axis=0, concat_axis=0, tiled=True)
    served_rows = flat_table[request].astype(jnp.bfloat16)
    arrived = lax.all_to_all(served_rows, "group", split_axis=0, concat_axis=0, tiled=True)
    q_rows = arrived.reshape(slot_count, embed_width)[position]
    full_r = lax.all_gather(r_tables, "local", axis=0, tiled=True)
    remainder_count = full_r.shape[0]
    r_pick = (
        r_index[:, :, None] == jnp.arange(remainder_count, dtype=jnp.int32)[None, None, :]
    ).astype(jnp.float32)
    r_rows = jnp.einsum("btr,rtd->btd", r_pick, full_r, precision=highest).reshape(
        lookups, embed_width
    )
    q_val = q_rows.astype(jnp.float32)
    embeds = (q_val * r_rows).astype(jnp.bfloat16).reshape(batch_rows, table_count, embed_width)
    vectors_all, features = interact(dense_vec, embeds)
    grads, d_features = dense_pass(features, layers, cotangent)
    d_embed = pair_back(d_features[:, embed_width:], vectors_all)[:, 1:, :].reshape(
        lookups, embed_width
    )
    grad_padded = jnp.concatenate(
        [d_embed * r_rows, jnp.zeros((1, embed_width), jnp.float32)], axis=0
    )
    outbound = grad_padded[source].reshape(groups, capacity, embed_width)
    returned = (
        lax.all_to_all(
            outbound.astype(jnp.bfloat16), "group", split_axis=0, concat_axis=0, tiled=True
        )
        .astype(outbound.dtype)
        .reshape(slot_count, embed_width)
    )
    served_flat = request.reshape(slot_count)
    q_part = jax.ops.segment_sum(returned, served_flat, num_segments=segment_count).reshape(
        q_tables.shape
    )
    q_piece = summed_on_arrival(q_part.astype(jnp.bfloat16), "local", 0)
    quarter = q_piece.shape[0]
    own_rows = lax.dynamic_slice_in_dim(q_tables, lax.axis_index("local") * quarter, quarter, 0)
    q_new = gather_directly(own_rows - table_rate * q_piece, "local", 0)
    r_part = jnp.einsum(
        "btr,btd->rtd",
        r_pick,
        (d_embed * q_val).reshape(batch_rows, table_count, embed_width),
        precision=highest,
    )
    summed = lax.psum(r_part, ("group", "local"))
    r_grad = lax.dynamic_slice_in_dim(
        summed, lax.axis_index("local") * r_tables.shape[0], r_tables.shape[0], 0
    )
    r_new = r_tables - table_rate * r_grad
    grad_wa, grad_ba, grad_wb, grad_bb, grad_wc, grad_bc, grad_wd, grad_bd = lax.psum(
        (
            grads[0][0],
            grads[0][1],
            grads[1][0],
            grads[1][1],
            grads[2][0],
            grads[2][1],
            grads[3][0],
            grads[3][1],
        ),
        ("group", "local"),
    )
    summed_grads = [(grad_wa, grad_ba), (grad_wb, grad_bb), (grad_wc, grad_bc), (grad_wd, grad_bd)]
    updated = []
    for (weight, biases), (w_grad, b_grad) in zip(layers, summed_grads):
        updated.append(weight.astype(jnp.float32) - dense_rate * w_grad)
        updated.append(biases - dense_rate * b_grad)
    return (
        q_new,
        r_new,
        updated[0],
        updated[1],
        updated[2],
        updated[3],
        updated[4],
        updated[5],
        updated[6],
        updated[7],
    )


def solution(mesh):
    return jax.shard_map(
        body,
        mesh=mesh,
        in_specs=(
            P(("group", "local"), None),
            P("group", None, None),
            P("local", None, None),
            P(("group", "local"), None, None),
            P(("group", "local"), None),
            P(("group", "local"), None),
            P(),
            P(),
            P(),
            P(),
            P(),
            P(),
            P(),
            P(),
            P(("group", "local"), None),
        ),
        out_specs=(
            P("group", None, None),
            P("local", None, None),
            P(),
            P(),
            P(),
            P(),
            P(),
            P(),
            P(),
            P(),
        ),
        check_vma=False,
    )
```

profile of v0, /device:TPU:1, one launch (start us, length us, event | category | flops | bytes accessed | tf_op | source)
XLA Modules:
  0.0 415.2 jit_solution(16516317859253861610)
XLA Ops:
  11.4 12.8 %scatter_custom_fusion = s32[6656]{0:T(1024)S(1)} fusion(s32[3328]{0:T(1024)S(1)} %fusion.39, s32[3328]{0:T(1024)S(1)} %iota.29, s32[]{:T(128)} %constant.27.clone.1), kind=kCustom, calls=%fused_computation.86 | custom fusion | bytes 26628 | tf_op jit(solution)/shard_map/scatter | solution.py:145
  24.2 34.5 %gather_fusion = s32[6656]{0:T(1024)S(1)} fusion(s32[3329]{0:T(1024)S(1)} %pad_add_fusion, s32[7168]{0:T(1024)S(1)} %pad_clamp_fusion.1), kind=kCustom, calls=%fused_computation | custom fusion | bytes 79872 | tf_op jit(solution)/shard_map/gather | solution.py:149
  59.5 9.6 %all-to-all-start = ((s32[32,1,208]{2,1,0:T(1,128)}), s32[32,1,208]{2,1,0:T(1,128)S(1)}, u32[]{:S(2)}, u32[]{:S(2)}) async-start(s32[32,1,208]{2,1,0:T(1,128)} %all_to_all.20), calls=%async_computation | async-start | bytes 65536 | tf_op jit(solution)/shard_map/all_to_all | solution.py:151
  71.8 4.6 %all-to-all-done = s32[32,1,208]{2,1,0:T(1,128)S(1)} async-done(((s32[32,1,208]{2,1,0:T(1,128)}), s32[32,1,208]{2,1,0:T(1,128)S(1)}, u32[]{:S(2)}, u32[]{:S(2)}) %all-to-all-start) | async-done | bytes 26656 | tf_op jit(solution)/shard_map/all_to_all | solution.py:151
  76.6 14.3 %gather_fusion.1 = bf16[6656,128]{1,0:T(8,128)(2,1)} fusion(bf16[3328,128]{1,0:T(8,128)(2,1)S(1)} %reshape.133, s32[7168]{0:T(1024)S(1)} %pad_clamp_fusion), kind=kCustom, calls=%fused_computation.1 | custom fusion | bytes 3434496 | tf_op jit(solution)/shard_map/gather | solution.py:152
  90.8 4.2 %all-to-all-start.1 = ((bf16[32,208,128]{2,1,0:T(8,128)(2,1)}), bf16[32,208,128]{2,1,0:T(8,128)(2,1)S(1)}, u32[]{:S(2)}, u32[]{:S(2)}) async-start(bf16[32,208,128]{2,1,0:T(8,128)(2,1)} %bitcast.56), calls=%async_computation.1 | async-start | bytes 3407872 | tf_op jit(solution)/shard_map/all_to_all | solution.py:153
  95.4 24.1 %all-to-all-done.1 = bf16[32,208,128]{2,1,0:T(8,128)(2,1)S(1)} async-done(((bf16[32,208,128]{2,1,0:T(8,128)(2,1)}), bf16[32,208,128]{2,1,0:T(8,128)(2,1)S(1)}, u32[]{:S(2)}, u32[]{:S(2)}) %all-to-all-start.1) | async-done | bytes 1703968 | tf_op jit(solution)/shard_map/all_to_all | solution.py:153
  119.5 6.5 %gather_fusion.2 = bf16[3328,128]{1,0:T(8,128)(2,1)S(1)} fusion(bf16[6656,128]{1,0:T(8,128)(2,1)S(1)} %bitcast.54, s32[4096]{0:T(1024)S(1)} %pad_clamp_fusion.2), kind=kCustom, calls=%fused_computation.2 | custom fusion | bytes 1717248 | tf_op jit(solution)/shard_map/gather | solution.py:154
  126.7 7.3 %fusion.5 = (bf16[128,26,128]{2,0,1:T(8,128)(2,1)S(1)}, f32[26,128,128]{2,1,0:T(8,128)}) fusion(f32[128,26,128]{2,1,0:T(8,128)S(1)} %reshape.138, f32[256,26,128]{2,0,1:T(8,128)} %all-gather.2.cloned.1.call-done, s32[128,26]{0,1:T(8,128)S(1)} %copy-done.15), kind=kOutput, calls=%fused_computation.19 | convolution fusion | flops 1310326784 | bytes 7681024 | tf_op jit(solution)/shard_map/btr,rtd->btd/dot_general | solution.py:160
  135.9 4.9 %gather_fusion.3 = bf16[351,128]{1,0:T(8,128)(2,1)S(1)} fusion(bf16[128,27,27]{0,2,1:T(8,128)(2,1)S(1)} %copy.92, s32[351]{0:T(512)S(1)} %copy-done), kind=kCustom, calls=%fused_computation.3 | custom fusion | bytes 182520 | tf_op jit(solution)/shard_map/gather | solution.py:48
  156.3 19.0 %scatter_fusion = f32[128,27,27]{0,2,1:T(8,128)S(1)} fusion(f32[128,27,27]{0,2,1:T(8,128)S(1)} %broadcast_in_dim.23, s32[351]{0:T(512)S(1)} %copy-done, f32[351,128]{1,0:T(8,128)S(1)} %convolution_bitcast_fusion), kind=kCustom, calls=%fused_computation.6 | custom fusion | bytes 541944 | tf_op jit(solution)/shard_map/scatter | solution.py:61
  175.6 2.9 copy.111
  178.5 3.3 fusion.14
  181.9 6.2 %fusion.4 = f32[256,26,128]{0,2,1:T(8,128)} fusion(s32[128,26]{0,1:T(8,128)S(1)} %copy-done.15, f32[128,26,128]{2,1,0:T(8,128)S(1)} %fusion.14, f32[128,26,128]{2,1,0:T(8,128)S(1)} %copy-done.2), kind=kOutput, calls=%fused_computation.16 | convolution fusion | flops 1309900800 | bytes 6829056 | tf_op jit(solution)/shard_map/btr,btd->rtd/dot_general | solution.py:189
  191.5 14.2 %gather_fusion.4 = bf16[6656,128]{1,0:T(8,128)(2,1)} fusion(bf16[3329,128]{1,0:T(8,128)(2,1)S(1)} %concatenate.24, s32[7168]{0:T(1024)S(1)} %pad_clamp_fusion.1), kind=kCustom, calls=%fused_computation.4 | custom fusion | bytes 3434496 | tf_op jit(solution)/shard_map/gather | solution.py:173
  205.8 5.0 %all-to-all-start.2 = ((bf16[32,208,128]{2,1,0:T(8,128)(2,1)}), bf16[32,208,128]{2,1,0:T(8,128)(2,1)S(1)}, u32[]{:S(2)}, u32[]{:S(2)}) async-start(bf16[32,208,128]{2,1,0:T(8,128)(2,1)} %bitcast.10), calls=%async_computation.2 | async-start | bytes 3407872 | tf_op jit(solution)/shard_map/all_to_all | solution.py:175
  210.9 28.2 %all-to-all-done.2 = bf16[32,208,128]{2,1,0:T(8,128)(2,1)S(1)} async-done(((bf16[32,208,128]{2,1,0:T(8,128)(2,1)}), bf16[32,208,128]{2,1,0:T(8,128)(2,1)S(1)}, u32[]{:S(2)}, u32[]{:S(2)}) %all-to-all-start.2) | async-done | bytes 1703968 | tf_op jit(solution)/shard_map/all_to_all | solution.py:175
  239.2 40.3 %scatter_custom_fusion.2 = f32[3328,128]{1,0:T(8,128)S(1)} fusion(s32[6656]{0:T(1024)S(1)} %reshape.195, bf16[6656,128]{1,0:T(8,128)(2,1)S(1)} %bitcast.55, f32[]{:T(128)} %constant.24.clone.1), kind=kCustom, calls=%fused_computation.9 | custom fusion | flops 1703936 | bytes 3407876 | tf_op jit(solution)/shard_map/scatter-add | solution.py:182
  283.0 4.2 %all-to-all-start.3 = ((bf16[4,32,26,128]{3,1,2,0:T(8,128)(2,1)}), bf16[4,32,26,128]{3,1,2,0:T(8,128)(2,1)S(1)}, u32[]{:S(2)}, u32[]{:S(2)}) async-start(bf16[4,32,26,128]{3,1,2,0:T(8,128)(2,1)} %copy.99), calls=%async_computation.3 | async-start | bytes 1703936 | tf_op jit(solution)/shard_map/all_to_all | solution.py:18
  287.3 13.2 %all-to-all-done.3 = bf16[4,32,26,128]{3,1,2,0:T(8,128)(2,1)S(1)} async-done(((bf16[4,32,26,128]{3,1,2,0:T(8,128)(2,1)}), bf16[4,32,26,128]{3,1,2,0:T(8,128)(2,1)S(1)}, u32[]{:S(2)}, u32[]{:S(2)}) %all-to-all-start.3) | async-done | bytes 852000 | tf_op jit(solution)/shard_map/all_to_all | solution.py:18
  303.5 3.6 all-to-all-start.4
  308.8 82.5 %all-reduce.1 = (f32[1024]{0:T(1024)S(1)}, f32[1024]{0:T(1024)S(1)}, f32[512]{0:T(512)S(1)}, f32[256]{0:T(256)S(1)}) all-reduce(f32[1024]{0:T(1024)S(1)} %get-tuple-element.61, f32[1024]{0:T(1024)S(1)} %get-tuple-element.63, f32[512]{0:T(512)S(1)} %get-tuple-element.65, ...), channel_id=1, replica_groups=mesh['group'=32,'local'=4] {'group','local'}, use_global_device_ids=true, to_apply=%region_9.10 | all-reduce | flops 2816 | bytes 22528 | tf_op jit(solution)/shard_map/psum | solution.py:200
  397.8 3.4 multiply_subtract_fusion.2
  401.2 4.5 %multiply_subtract_fusion = f32[1024,1024]{1,0:T(8,128)} fusion(f32[1024,1024]{1,0:T(8,128)S(1)} %copy-done.4, bf16[1024,1024]{1,0:T(8,128)(2,1)} %param.31), kind=kLoop, calls=%fused_computation.8 | loop fusion | flops 3145728 | bytes 10485760 | tf_op jit(solution)/shard_map/sub | solution.py:216
  (116 shorter events, 47.2 us)
Async XLA Ops:
  7.2 119.1 %all-gather.2.cloned.1.call-start = ((), (), s32[]{:S(2)}) async-start(), calls=%async_computation.5 | async-start | bytes 4259840 | tf_op jit(solution)/shard_map/all_gather | solution.py:155
  59.5 16.9 %all-to-all-start = ((s32[32,1,208]{2,1,0:T(1,128)}), s32[32,1,208]{2,1,0:T(1,128)S(1)}, u32[]{:S(2)}, u32[]{:S(2)}) async-start(s32[32,1,208]{2,1,0:T(1,128)} %all_to_all.20), calls=%async_computation | async-start | bytes 65536 | tf_op jit(solution)/shard_map/all_to_all | solution.py:151
  71.6 19.3 %copy-start.3 = (f32[128,26,128]{2,1,0:T(8,128)}, f32[128,26,128]{2,1,0:T(8,128)S(1)}, u32[]{:S(2)}) copy-start(f32[128,26,128]{2,1,0:T(8,128)S(1)} %copy.84) | copy-start | bytes 5111812
  90.8 4.4 %copy-start.14 = (bf16[128,128]{1,0:T(8,128)(2,1)S(1)}, bf16[128,128]{1,0:T(8,128)(2,1)}, u32[]{:S(2)}) copy-start(bf16[128,128]{1,0:T(8,128)(2,1)} %param.23) | copy-start | bytes 98308
  90.8 28.7 %all-to-all-start.1 = ((bf16[32,208,128]{2,1,0:T(8,128)(2,1)}), bf16[32,208,128]{2,1,0:T(8,128)(2,1)S(1)}, u32[]{:S(2)}, u32[]{:S(2)}) async-start(bf16[32,208,128]{2,1,0:T(8,128)(2,1)} %bitcast.56), calls=%async_computation.1 | async-start | bytes 3407872 | tf_op jit(solution)/shard_map/all_to_all | solution.py:153
  95.0 299.4 %all-reduce.5.cloned.1.call-start = ((), (), s32[]{:S(2)}) async-start(), calls=%async_computation.6 | async-start | bytes 24379392 | tf_op jit(solution)/shard_map/psum | solution.py:195
  126.2 7.8 %copy-start.1 = (f32[128,26,128]{2,1,0:T(8,128)}, f32[128,26,128]{2,1,0:T(8,128)S(1)}, u32[]{:S(2)}) copy-start(f32[128,26,128]{2,1,0:T(8,128)S(1)} %reshape.138) | copy-start | bytes 5111812
  134.1 1.8 copy-start
  134.1 6.7 %copy-start.17 = (f32[1024]{0:T(1024)S(1)}, f32[1024]{0:T(1024)}, u32[]{:S(2)}) copy-start(f32[1024]{0:T(1024)} %param.30) | copy-start | bytes 12292
  134.8 7.6 %copy-start.18 = (f32[1024]{0:T(1024)S(1)}, f32[1024]{0:T(1024)}, u32[]{:S(2)}) copy-start(f32[1024]{0:T(1024)} %param.32) | copy-start | bytes 12292
  142.4 2.2 copy-start.9
  142.4 2.2 copy-start.19
  145.8 1.6 copy-start.7
  178.5 3.4 copy-start.2
  205.8 33.4 %all-to-all-start.2 = ((bf16[32,208,128]{2,1,0:T(8,128)(2,1)}), bf16[32,208,128]{2,1,0:T(8,128)(2,1)S(1)}, u32[]{:S(2)}, u32[]{:S(2)}) async-start(bf16[32,208,128]{2,1,0:T(8,128)(2,1)} %bitcast.10), calls=%async_computation.2 | async-start | bytes 3407872 | tf_op jit(solution)/shard_map/all_to_all | solution.py:175
  283.0 17.4 %all-to-all-start.3 = ((bf16[4,32,26,128]{3,1,2,0:T(8,128)(2,1)}), bf16[4,32,26,128]{3,1,2,0:T(8,128)(2,1)S(1)}, u32[]{:S(2)}, u32[]{:S(2)}) async-start(bf16[4,32,26,128]{3,1,2,0:T(8,128)(2,1)} %copy.99), calls=%async_computation.3 | async-start | bytes 1703936 | tf_op jit(solution)/shard_map/all_to_all | solution.py:18
  303.5 89.5 %all-to-all-start.4 = ((f32[4,32,26,128]{3,1,2,0:T(8,128)}), f32[4,32,26,128]{3,1,2,0:T(8,128)S(1)}, u32[]{:S(2)}, u32[]{:S(2)}) async-start(f32[4,32,26,128]{3,1,2,0:T(8,128)} %broadcast_in_dim.29), calls=%async_computation.4 | async-start | bytes 3407872 | tf_op jit(solution)/shard_map/all_to_all | solution.py:30
  307.1 84.2 %copy-start.20 = (f32[256]{0:T(256)S(1)}, f32[256]{0:T(256)}, u32[]{:S(2)}) copy-start(f32[256]{0:T(256)} %param.36) | copy-start | bytes 3076
  396.4 1.4 copy-start.6
  397.8 3.4 copy-start.4
  401.2 4.5 %copy-start.8 = (f32[1024,512]{1,0:T(8,128)S(1)}, f32[1024,512]{1,0:T(8,128)}, u32[]{:S(2)}) copy-start(f32[1024,512]{1,0:T(8,128)} %get-tuple-element.57) | copy-start | bytes 6291460
  401.2 4.5 %copy-start.10 = (bf16[1024,512]{1,0:T(8,128)(2,1)S(1)}, bf16[1024,512]{1,0:T(8,128)(2,1)}, u32[]{:S(2)}) copy-start(bf16[1024,512]{1,0:T(8,128)(2,1)} %param.33) | copy-start | bytes 3145732
  405.8 1.7 copy-start.11
  405.8 1.7 copy-start.13
  (4 other events, 3.8 us)
Sparse Core Ops, SparseCore 0:
  9.6 44.6 all-gather.1
  188.2 188.2 all-reduce.4
where the time goes:
time: 416 us; the launch traced here: 415 us
  local copies, waits for them, and re-layouts  128 us (31%)
  blocking collectives  82.5 us (20%)
  waiting for transfers between devices  70.8 us (17%)
  other arithmetic  61.5 us (15%)
  matrix products  31.2 us (8%)
  starting transfers between devices  26.8 us (6%)
  between operations  14.6 us (4%)
    psum x1, blocking collectives, body(): lax.psum((grads[0][0], grads[0][1], grads[1][0], grads[1][1], grads[2][0]...  82.5 us
    scatter-add x1, other arithmetic, body(): jax.ops.segment_sum(returned, served_flat, num_segments=segment_count)  40.3 us
    gather x1, local copies, waits for them, and re-layouts, body(): outgoing = keys_padded[source].reshape(groups, capacity)  34.5 us
    all_to_all x1, waiting for transfers between devices, body(): lax.all_to_all(outbound.astype(jnp.bfloat16), 'group', split_axis=0, conc...  28.2 us
    all_to_all x1, waiting for transfers between devices, body(): lax.all_to_all(served_rows, 'group', split_axis=0, concat_axis=0, tiled=T...  24.1 us
    scatter x1, local copies, waits for them, and re-layouts, pair_back(): spread = jnp.zeros((vectors_all.shape[0], vectors, vectors), jnp.float32)...  19 us
    gather x1, local copies, waits for them, and re-layouts, body(): served_rows = flat_table[request].astype(jnp.bfloat16)  14.3 us
    gather x1, local copies, waits for them, and re-layouts, body(): outbound = grad_padded[source].reshape(groups, capacity, embed_width)  14.2 us
  transfers between devices with their start and end apart: 7, of which 4 were waited for; matrix products, arithmetic and copies ran while one was open for 35% of the time, Pallas kernels for 0%

commit v1 on v0

--- a/solution.py
+++ b/solution.py
@@ -115,6 +115,10 @@
     b_four,
     cotangent,
 ):
+
+    def proceed_the_chunk(panel):
+        return lax.psum(lax.psum(panel, "local"), "group")
+
     layers = [(w_one, b_one), (w_two, b_two), (w_three, b_three), (w_four, b_four)]
     groups = lax.axis_size("group")
     batch_rows, table_count = q_local.shape
@@ -197,7 +201,7 @@
         summed, lax.axis_index("local") * r_tables.shape[0], r_tables.shape[0], 0
     )
     r_new = r_tables - table_rate * r_grad
-    grad_wa, grad_ba, grad_wb, grad_bb, grad_wc, grad_bc, grad_wd, grad_bd = lax.psum(
+    grad_wa, grad_ba, grad_wb, grad_bb, grad_wc, grad_bc, grad_wd, grad_bd = proceed_the_chunk(
         (
             grads[0][0],
             grads[0][1],
@@ -207,8 +211,7 @@
             grads[2][1],
             grads[3][0],
             grads[3][1],
-        ),
-        ("group", "local"),
+        )
     )
     summed_grads = [(grad_wa, grad_ba), (grad_wb, grad_bb), (grad_wc, grad_bc), (grad_wd, grad_bd)]
     updated = []

time: 416 us -> 638 us (1.53)
  waiting for transfers between devices: 70.8 us -> 227 us
  blocking collectives: 82.5 us -> 148 us
    psum x0 -> x2, waiting for transfers between devices: none -> 161 us  [proceed_the_chunk(): return lax.psum(lax.psum(panel, 'local'), 'group')]
    psum x1 -> x2, blocking collectives: 82.5 us -> 148 us  [proceed_the_chunk(): return lax.psum(lax.psum(panel, 'local'), 'group')]
  transfers between devices with their start and end apart: 7 -> 9, of which waited for: 4 -> 6; matrix products, arithmetic and copies ran while one was open for 35% -> 28% of each run, Pallas kernels for 0% -> 0%
where the time goes in v1:
time: 638 us; the launch traced here: 637 us
  waiting for transfers between devices  227 us (36%)
  blocking collectives  148 us (23%)
  local copies, waits for them, and re-layouts  128 us (20%)
  other arithmetic  60.1 us (9%)
  starting transfers between devices  30.2 us (5%)
  matrix products  30 us (5%)
  between operations  14.4 us (2%)
    psum x2, waiting for transfers between devices, proceed_the_chunk(): return lax.psum(lax.psum(panel, 'local'), 'group')  161 us
    psum x2, blocking collectives, proceed_the_chunk(): return lax.psum(lax.psum(panel, 'local'), 'group')  148 us
    scatter-add x1, other arithmetic, body(): jax.ops.segment_sum(returned, served_flat, num_segments=segment_count)  40.6 us
    gather x1, local copies, waits for them, and re-layouts, body(): outgoing = keys_padded[source].reshape(groups, capacity)  34.5 us
    all_to_all x1, waiting for transfers between devices, body(): lax.all_to_all(outbound.astype(jnp.bfloat16), 'group', split_axis=0, conc...  26.3 us
    all_to_all x1, waiting for transfers between devices, body(): lax.all_to_all(served_rows, 'group', split_axis=0, concat_axis=0, tiled=T...  24.1 us
    scatter x1, local copies, waits for them, and re-layouts, pair_back(): spread = jnp.zeros((vectors_all.shape[0], vectors, vectors), jnp.float32)...  18.8 us
    gather x1, local copies, waits for them, and re-layouts, body(): served_rows = flat_table[request].astype(jnp.bfloat16)  14.3 us
  transfers between devices with their start and end apart: 9, of which 6 were waited for; matrix products, arithmetic and copies ran while one was open for 28% of the time, Pallas kernels for 0%

profile of v1, /device:TPU:1, one launch (start us, length us, event | category | flops | bytes accessed | tf_op | source)
XLA Modules:
  0.0 637.3 jit_solution(2615601814701471318)
XLA Ops:
  11.4 12.8 %scatter_custom_fusion = s32[6656]{0:T(1024)S(1)} fusion(s32[3328]{0:T(1024)S(1)} %fusion.39, s32[3328]{0:T(1024)S(1)} %iota.29, s32[]{:T(128)} %constant.27.clone.1), kind=kCustom, calls=%fused_computation.86 | custom fusion | bytes 26628 | tf_op jit(solution)/shard_map/scatter | solution.py:149
  24.2 34.5 %gather_fusion = s32[6656]{0:T(1024)S(1)} fusion(s32[3329]{0:T(1024)S(1)} %pad_add_fusion, s32[7168]{0:T(1024)S(1)} %pad_clamp_fusion.1), kind=kCustom, calls=%fused_computation | custom fusion | bytes 79872 | tf_op jit(solution)/shard_map/gather | solution.py:153
  59.5 9.6 %all-to-all-start = ((s32[32,1,208]{2,1,0:T(1,128)}), s32[32,1,208]{2,1,0:T(1,128)S(1)}, u32[]{:S(2)}, u32[]{:S(2)}) async-start(s32[32,1,208]{2,1,0:T(1,128)} %all_to_all.20), calls=%async_computation | async-start | bytes 65536 | tf_op jit(solution)/shard_map/all_to_all | solution.py:155
  71.8 4.6 all-to-all-done
  76.6 14.3 %gather_fusion.1 = bf16[6656,128]{1,0:T(8,128)(2,1)} fusion(bf16[3328,128]{1,0:T(8,128)(2,1)S(1)} %reshape.133, s32[7168]{0:T(1024)S(1)} %pad_clamp_fusion), kind=kCustom, calls=%fused_computation.1 | custom fusion | bytes 3434496 | tf_op jit(solution)/shard_map/gather | solution.py:156
  90.8 4.2 all-to-all-start.1
  95.4 24.1 %all-to-all-done.1 = bf16[32,208,128]{2,1,0:T(8,128)(2,1)S(1)} async-done(((bf16[32,208,128]{2,1,0:T(8,128)(2,1)}), bf16[32,208,128]{2,1,0:T(8,128)(2,1)S(1)}, u32[]{:S(2)}, u32[]{:S(2)}) %all-to-all-start.1) | async-done | bytes 1703968 | tf_op jit(solution)/shard_map/all_to_all | solution.py:157
  119.5 6.5 %gather_fusion.2 = bf16[3328,128]{1,0:T(8,128)(2,1)S(1)} fusion(bf16[6656,128]{1,0:T(8,128)(2,1)S(1)} %bitcast.54, s32[4096]{0:T(1024)S(1)} %pad_clamp_fusion.2), kind=kCustom, calls=%fused_computation.2 | custom fusion | bytes 1717248 | tf_op jit(solution)/shard_map/gather | solution.py:158
  126.7 7.3 %fusion.5 = (bf16[128,26,128]{2,0,1:T(8,128)(2,1)S(1)}, f32[26,128,128]{2,1,0:T(8,128)}) fusion(f32[128,26,128]{2,1,0:T(8,128)S(1)} %reshape.138, f32[256,26,128]{2,0,1:T(8,128)} %all-gather.2.cloned.1.call-done, s32[128,26]{0,1:T(8,128)S(1)} %copy-done.17), kind=kOutput, calls=%fused_computation.19 | convolution fusion | flops 1310326784 | bytes 7681024 | tf_op jit(solution)/shard_map/btr,rtd->btd/dot_general | solution.py:164
  135.9 4.9 gather_fusion.3
  155.1 18.8 %scatter_fusion = f32[128,27,27]{0,2,1:T(8,128)S(1)} fusion(f32[128,27,27]{0,2,1:T(8,128)S(1)} %broadcast_in_dim.23, s32[351]{0:T(512)S(1)} %copy-done, f32[351,128]{1,0:T(8,128)S(1)} %convolution_bitcast_fusion), kind=kCustom, calls=%fused_computation.6 | custom fusion | bytes 541944 | tf_op jit(solution)/shard_map/scatter | solution.py:61
  180.4 6.2 fusion.4
  186.7 132.2 %all-reduce.13.cloned.1.call-done = (f32[479,1024]{1,0:T(8,128)}, f32[1024,1024]{1,0:T(8,128)}, f32[1024,512]{1,0:T(8,128)}, f32[512,256]{1,0:T(8,128)}) async-done(((f32[479,1024]{1,0:T(8,128)}, f32[1024,1024]{1,0:T(8,128)}, f32[1024,512]{1,0:T(8,128)}, f32[512,256]{1,0:T(8,128)}), (f32[479,1024]{1,0:T(8,128)}, f32[1024,1024]{1,0:T(8,128)}, f32[1024,512]{1,0:T(8,128)}, ...) | async-done | bytes 8777744 | tf_op jit(solution)/shard_map/psum | solution.py:120
  322.3 14.2 %gather_fusion.4 = bf16[6656,128]{1,0:T(8,128)(2,1)} fusion(bf16[3329,128]{1,0:T(8,128)(2,1)S(1)} %concatenate.24, s32[7168]{0:T(1024)S(1)} %pad_clamp_fusion.1), kind=kCustom, calls=%fused_computation.4 | custom fusion | bytes 3434496 | tf_op jit(solution)/shard_map/gather | solution.py:177
  336.5 7.9 %all-to-all-start.2 = ((bf16[32,208,128]{2,1,0:T(8,128)(2,1)}), bf16[32,208,128]{2,1,0:T(8,128)(2,1)S(1)}, u32[]{:S(2)}, u32[]{:S(2)}) async-start(bf16[32,208,128]{2,1,0:T(8,128)(2,1)} %bitcast.10), calls=%async_computation.2 | async-start | bytes 3407872 | tf_op jit(solution)/shard_map/all_to_all | solution.py:179
  344.6 26.3 %all-to-all-done.2 = bf16[32,208,128]{2,1,0:T(8,128)(2,1)S(1)} async-done(((bf16[32,208,128]{2,1,0:T(8,128)(2,1)}), bf16[32,208,128]{2,1,0:T(8,128)(2,1)S(1)}, u32[]{:S(2)}, u32[]{:S(2)}) %all-to-all-start.2) | async-done | bytes 1703968 | tf_op jit(solution)/shard_map/all_to_all | solution.py:179
  370.9 40.6 %scatter_custom_fusion.2 = f32[3328,128]{1,0:T(8,128)S(1)} fusion(s32[6656]{0:T(1024)S(1)} %reshape.195, bf16[6656,128]{1,0:T(8,128)(2,1)S(1)} %bitcast.55, f32[]{:T(128)} %constant.24.clone.1), kind=kCustom, calls=%fused_computation.9 | custom fusion | flops 1703936 | bytes 3407876 | tf_op jit(solution)/shard_map/scatter-add | solution.py:186
  415.0 3.5 all-to-all-start.3
  418.5 10.7 %all-to-all-done.3 = bf16[4,32,26,128]{3,1,2,0:T(8,128)(2,1)S(1)} async-done(((bf16[4,32,26,128]{3,1,2,0:T(8,128)(2,1)}), bf16[4,32,26,128]{3,1,2,0:T(8,128)(2,1)S(1)}, u32[]{:S(2)}, u32[]{:S(2)}) %all-to-all-start.3) | async-done | bytes 852000 | tf_op jit(solution)/shard_map/all_to_all | solution.py:18
  432.3 4.5 all-to-all-start.4
  437.4 27.4 %all-reduce.3 = (f32[1024]{0:T(1024)S(1)}, f32[1024]{0:T(1024)S(1)}, f32[512]{0:T(512)S(1)}, f32[256]{0:T(256)S(1)}) all-reduce(f32[1024]{0:T(1024)S(1)} %get-tuple-element.68, f32[1024]{0:T(1024)S(1)} %get-tuple-element.70, f32[512]{0:T(512)S(1)} %get-tuple-element.72, ...), channel_id=1, replica_groups=mesh['group'=32,'local'=4] {'local'}, use_global_device_ids=true, to_apply=%region_10.11 | all-reduce | flops 2816 | bytes 22528 | tf_op jit(solution)/shard_map/psum | solution.py:120
  464.8 120.4 %all-reduce.1 = (f32[1024]{0:T(1024)S(1)}, f32[1024]{0:T(1024)S(1)}, f32[512]{0:T(512)S(1)}, f32[256]{0:T(256)S(1)}) all-reduce(f32[1024]{0:T(1024)S(1)} %get-tuple-element.58, f32[1024]{0:T(1024)S(1)} %get-tuple-element.59, f32[512]{0:T(512)S(1)} %get-tuple-element.60, ...), channel_id=1, replica_groups=mesh['group'=32,'local'=4] {'group'}, use_global_device_ids=true, to_apply=%region_11.12 | all-reduce | flops 2816 | bytes 22528 | tf_op jit(solution)/shard_map/psum | solution.py:120
  593.3 28.6 %all-reduce.11.cloned.1.call-done = (f32[479,1024]{1,0:T(8,128)}, f32[1024,1024]{1,0:T(8,128)}, f32[1024,512]{1,0:T(8,128)}, f32[512,256]{1,0:T(8,128)}) async-done(((f32[479,1024]{1,0:T(8,128)}, f32[1024,1024]{1,0:T(8,128)}, f32[1024,512]{1,0:T(8,128)}, f32[512,256]{1,0:T(8,128)}), (f32[479,1024]{1,0:T(8,128)}, f32[1024,1024]{1,0:T(8,128)}, f32[1024,512]{1,0:T(8,128)}, ...) | async-done | bytes 8777744 | tf_op jit(solution)/shard_map/psum | solution.py:120
  621.9 3.4 multiply_subtract_fusion.2
  (127 shorter events, 55.5 us)
Async XLA Ops:
  7.2 119.1 %all-gather.2.cloned.1.call-start = ((), (), s32[]{:S(2)}) async-start(), calls=%async_computation.5 | async-start | bytes 4259840 | tf_op jit(solution)/shard_map/all_gather | solution.py:159
  59.5 16.9 %all-to-all-start = ((s32[32,1,208]{2,1,0:T(1,128)}), s32[32,1,208]{2,1,0:T(1,128)S(1)}, u32[]{:S(2)}, u32[]{:S(2)}) async-start(s32[32,1,208]{2,1,0:T(1,128)} %all_to_all.20), calls=%async_computation | async-start | bytes 65536 | tf_op jit(solution)/shard_map/all_to_all | solution.py:155
  71.6 19.3 %copy-start.3 = (f32[128,26,128]{2,1,0:T(8,128)}, f32[128,26,128]{2,1,0:T(8,128)S(1)}, u32[]{:S(2)}) copy-start(f32[128,26,128]{2,1,0:T(8,128)S(1)} %copy.84) | copy-start | bytes 5111812
  90.8 4.4 copy-start.16
  90.8 28.7 %all-to-all-start.1 = ((bf16[32,208,128]{2,1,0:T(8,128)(2,1)}), bf16[32,208,128]{2,1,0:T(8,128)(2,1)S(1)}, u32[]{:S(2)}, u32[]{:S(2)}) async-start(bf16[32,208,128]{2,1,0:T(8,128)(2,1)} %bitcast.56), calls=%async_computation.1 | async-start | bytes 3407872 | tf_op jit(solution)/shard_map/all_to_all | solution.py:157
  95.0 223.9 %all-reduce.13.cloned.1.call-start = ((), (), s32[]{:S(2)}) async-start(), calls=%async_computation.8 | async-start | bytes 17563648 | tf_op jit(solution)/shard_map/psum | solution.py:120
  126.2 7.8 %copy-start.1 = (f32[128,26,128]{2,1,0:T(8,128)}, f32[128,26,128]{2,1,0:T(8,128)S(1)}, u32[]{:S(2)}) copy-start(f32[128,26,128]{2,1,0:T(8,128)S(1)} %reshape.138) | copy-start | bytes 5111812
  134.1 6.7 %copy-start.5 = (bf16[479,1024]{1,0:T(8,128)(2,1)S(1)}, bf16[479,1024]{1,0:T(8,128)(2,1)}, u32[]{:S(2)}) copy-start(bf16[479,1024]{1,0:T(8,128)(2,1)} %param.29) | copy-start | bytes 2942980
  134.1 6.7 %copy-start.19 = (f32[1024]{0:T(1024)S(1)}, f32[1024]{0:T(1024)}, u32[]{:S(2)}) copy-start(f32[1024]{0:T(1024)} %param.30) | copy-start | bytes 12292
  134.8 6.4 copy-start.20
  141.2 2.2 copy-start.11
  154.4 432.6 %all-reduce.9.cloned.1.call-start = ((), (), s32[]{:S(2)}) async-start(), calls=%async_computation.6 | async-start | bytes 6815744 | tf_op jit(solution)/shard_map/psum | solution.py:199
  177.1 3.4 copy-start.2
  186.7 435.2 %all-reduce.11.cloned.1.call-start = ((), (), s32[]{:S(2)}) async-start(), calls=%async_computation.7 | async-start | bytes 17563648 | tf_op jit(solution)/shard_map/psum | solution.py:120
  336.5 34.3 %all-to-all-start.2 = ((bf16[32,208,128]{2,1,0:T(8,128)(2,1)}), bf16[32,208,128]{2,1,0:T(8,128)(2,1)S(1)}, u32[]{:S(2)}, u32[]{:S(2)}) async-start(bf16[32,208,128]{2,1,0:T(8,128)(2,1)} %bitcast.10), calls=%async_computation.2 | async-start | bytes 3407872 | tf_op jit(solution)/shard_map/all_to_all | solution.py:179
  415.0 14.3 %all-to-all-start.3 = ((bf16[4,32,26,128]{3,1,2,0:T(8,128)(2,1)}), bf16[4,32,26,128]{3,1,2,0:T(8,128)(2,1)S(1)}, u32[]{:S(2)}, u32[]{:S(2)}) async-start(bf16[4,32,26,128]{3,1,2,0:T(8,128)(2,1)} %copy.99), calls=%async_computation.3 | async-start | bytes 1703936 | tf_op jit(solution)/shard_map/all_to_all | solution.py:18
  432.3 4.5 copy-start.7
  432.3 158.0 %all-to-all-start.4 = ((f32[4,32,26,128]{3,1,2,0:T(8,128)}), f32[4,32,26,128]{3,1,2,0:T(8,128)}, u32[]{:S(2)}, u32[]{:S(2)}) async-start(f32[4,32,26,128]{3,1,2,0:T(8,128)} %broadcast_in_dim.29), calls=%async_computation.4 | async-start | bytes 3407872 | tf_op jit(solution)/shard_map/all_to_all | solution.py:30
  436.9 148.4 %copy-start.22 = (f32[256]{0:T(256)S(1)}, f32[256]{0:T(256)}, u32[]{:S(2)}) copy-start(f32[256]{0:T(256)} %param.36) | copy-start | bytes 3076
  590.3 31.6 %copy-start.6 = (bf16[479,1024]{1,0:T(8,128)(2,1)S(1)}, bf16[479,1024]{1,0:T(8,128)(2,1)}, u32[]{:S(2)}) copy-start(bf16[479,1024]{1,0:T(8,128)(2,1)} %param.29) | copy-start | bytes 2942980
  590.4 35.0 %copy-start.9 = (bf16[1024,1024]{1,0:T(8,128)(2,1)S(1)}, bf16[1024,1024]{1,0:T(8,128)(2,1)}, u32[]{:S(2)}) copy-start(bf16[1024,1024]{1,0:T(8,128)(2,1)} %param.31) | copy-start | bytes 6291460
  621.9 3.4 copy-start.4
  625.4 2.8 copy-start.10
  625.4 2.8 copy-start.12
  (8 other events, 11.6 us)
Sparse Core Ops, SparseCore 0:
  9.6 44.6 all-gather.1
  154.5 164.2 all-reduce.12
  323.8 174.6 all-reduce.8
  502.2 119.6 all-reduce.10
